TPU v7x, 32 devices: a whole 2x2x4 slice. The times are simulated.
32 devices in a mesh: dp: 2 (over y), ep: 16 (over z, x, core).
Axes of the slice: x: 2, y: 2, z: 4, core: 2. Of those that a mesh axis runs over, the one named last changes fastest.
Arguments:
- tokens: bfloat16 [3072, 2048], P(('dp', 'ep')), parts along dimension 0, may hold values from -6 to 6
- routes: int32 [3072, 8], P(('dp', 'ep')), parts along dimension 0, may hold values from 0 to 15, all different within a row; in each aligned block of 96 rows (0 to 95, 96 to 191, ...) at most 72 rows name the same one
- combine_weights: bfloat16 [3072, 8], P(('dp', 'ep')), parts along dimension 0, may hold values from 0.049804688 to 1
- w_gate: bfloat16 [16, 2048, 768], P('ep'), may hold values from -0.125 to 0.125
- w_up: bfloat16 [16, 2048, 768], P('ep'), may hold values from -0.125 to 0.125
- w_down: bfloat16 [16, 768, 2048], P('ep'), may hold values from -0.21875 to 0.21875
Outputs:
- mixed: bfloat16 [3072, 2048], P(('dp', 'ep')), parts along dimension 0
There are 2 independent parts, one for each index of `dp`. A program takes and returns all parts, laid end to end along the dimension named above; an argument that names none is the same for every part. Nothing has to cross between parts.
Inputs may be any that keep to these rules, and one draw needn't show every extreme that they name: `routes`: each row names 8 different experts. Among the 96 rows of one device no expert is named by more than 72 rows, a bound that some blocks reach.
All inputs are finite; a program needn't handle non-finite values.
Results may differ from a plain program's by a relative error of at most 0.012.
Values may be sent and summed in bfloat16 or wider, within the bound.
A program may use at most 128 MiB of HBM per device.

v0:
```python
import jax
import jax.numpy as jnp
from jax import lax
from jax.sharding import PartitionSpec as P


def expert_ffn(rows, row_weight, gate_matrix, upward_matrix, down_matrix):
    gate = jnp.dot(rows, gate_matrix, preferred_element_type=jnp.float32)
    upward = jnp.dot(rows, upward_matrix, preferred_element_type=jnp.float32)
    hidden = (jax.nn.silu(gate) * upward).astype(jnp.bfloat16)
    result = jnp.dot(hidden, down_matrix, preferred_element_type=jnp.float32)
    return (result * row_weight.astype(jnp.float32)[:, None]).astype(jnp.bfloat16)


def run_expert(arrived, arrived_weight, gate_matrix, upward_matrix, down_matrix):
    sources, slots, width = arrived.shape
    rows = arrived.reshape(sources * slots, width)
    row_weight = arrived_weight.reshape(sources * slots)
    output = expert_ffn(rows, row_weight, gate_matrix, upward_matrix, down_matrix)
    return output.reshape(sources, slots, width)


def local(tokens, routes, combine_weights, w_gate, w_up, w_down):
    peers = lax.axis_size("ep")
    local_tokens, width = tokens.shape
    top_count = routes.shape[1]
    room = min(local_tokens, 3 * local_tokens * top_count // (2 * peers))
    pair_count = local_tokens * top_count
    flat_routes = routes.reshape(-1)
    one_hot = (flat_routes[:, None] == jnp.arange(peers, dtype=jnp.int32)[None, :]).astype(
        jnp.int32
    )
    earlier = jnp.cumsum(one_hot, axis=0) - one_hot
    position = jnp.sum(earlier * one_hot, axis=1)
    slot_index = flat_routes * room + position
    owner = jnp.full((peers * room,), pair_count, jnp.int32)
    owner = owner.at[slot_index].set(jnp.arange(pair_count, dtype=jnp.int32))
    send_rows = jnp.take(tokens, owner // top_count, axis=0, mode="fill", fill_value=0)
    send_rows = send_rows.reshape(peers, room, width)
    send_weight = jnp.take(combine_weights.reshape(-1), owner, mode="fill", fill_value=0)
    send_weight = send_weight.reshape(peers, room)
    gate_matrix = w_gate[0]
    upward_matrix = w_up[0]
    down_matrix = w_down[0]
    arrived, arrived_weight = (
        lax.all_to_all(send_rows, "ep", split_axis=0, concat_axis=0, tiled=True),
        lax.all_to_all(send_weight, "ep", split_axis=0, concat_axis=0, tiled=True),
    )
    output = run_expert(arrived, arrived_weight, gate_matrix, upward_matrix, down_matrix)
    back = lax.all_to_all(output, "ep", split_axis=0, concat_axis=0, tiled=True)
    back_rows = back.reshape(peers * room, width)
    per_pair = jnp.take(back_rows, slot_index, axis=0)
    summed = jnp.sum(per_pair.reshape(local_tokens, top_count, width).astype(jnp.float32), axis=1)
    return summed.astype(jnp.bfloat16)


def solution(mesh):
    in_specs = (
        P(("dp", "ep"), None),
        P(("dp", "ep"), None),
        P(("dp", "ep"), None),
        P("ep", None, None),
        P("ep", None, None),
        P("ep", None, None),
    )
    out_specs = P(("dp", "ep"), None)
    return jax.shard_map(local, mesh=mesh, in_specs=in_specs, out_specs=out_specs, check_vma=False)
```

profile of v0, /device:TPU:15, one launch (start us, length us, event | category | flops | bytes accessed | tf_op | source)
XLA Modules:
  0.0 301.9 jit_solution(1800303695094019725)
XLA Ops:
  0.0 1.6 copy.19
  1.6 0.9 eq.26
  2.4 1.5 reshape.124
  3.9 0.7 broadcast_multiply_fusion
  4.6 0.6 fusion.10
  5.2 4.1 %reduce-window.6 = s32[16,6,128]{2,0,1:T(8,128)} reduce-window(s32[16,6,128]{2,0,1:T(8,128)} %fusion.10, s32[]{:T(128)} %constant.61.clone.1), window={size=1x1x128 pad=0_0x0_0x127_0}, to_apply=%region_0.0 | reduce-window | flops 1560576 | bytes 98308 | tf_op jit(solution)/shard_map/reduce-window
  9.4 1.0 slice_reduce_fusion
  10.4 0.7 copy.24
  11.1 0.9 mul.40
  12.0 0.9 fusion.9
  13.6 3.5 %scatter_custom_fusion = s32[1152]{0:T(1024)S(1)} fusion(s32[768]{0:T(1024)S(1)} %fusion.15, s32[768]{0:T(1024)} %iota.11, s32[]{:T(128)} %constant.64.clone.1), kind=kCustom, calls=%fused_computation.41 | custom fusion | bytes 5120 | tf_op jit(solution)/shard_map/scatter | solution.py:37
  17.1 0.6 pad_clamp_fusion
  17.7 1.4 copy.25
  19.1 0.8 reshape.127
  19.9 10.3 %gather_fusion.1 = bf16[1152]{0:T(1024)(128)(2,1)} fusion(bf16[768]{0:T(1024)(128)(2,1)S(1)} %reshape.127, s32[2048]{0:T(1024)} %pad_clamp_fusion), kind=kCustom, calls=%fused_computation.1 | custom fusion | bytes 9216 | tf_op jit(solution)/shard_map/jit(_take)/gather | solution.py:40
  30.2 0.7 and_select_fusion
  30.9 0.7 select_n.65
  31.6 6.5 %all-to-all-start.1 = ((bf16[16,1,72]{2,1,0:T(2,128)(2,1)}), bf16[16,1,72]{2,1,0:T(2,128)(2,1)}, u32[]{:S(2)}, u32[]{:S(2)}) async-start(bf16[16,1,72]{2,1,0:T(2,128)(2,1)} %select_n.65), calls=%async_computation.1 | async-start | bytes 16384 | tf_op jit(solution)/shard_map/all_to_all | solution.py:47
  38.2 0.6 compare_and_fusion
  38.8 0.8 broadcast_in_dim.40
  39.6 6.0 %gather_fusion = bf16[1152,2048]{1,0:T(8,128)(2,1)} fusion(bf16[96,2048]{1,0:T(8,128)(2,1)S(1)} %copy-done.1, s32[2048]{0:T(1024)S(1)} %pad_clamp_fusion.1), kind=kCustom, calls=%fused_computation | custom fusion | bytes 9441792 | tf_op jit(solution)/shard_map/jit(_take)/gather | solution.py:38
  45.6 4.9 %broadcast_select_fusion = bf16[16,72,2048]{2,1,0:T(8,128)(2,1)} fusion(bf16[16,72,2048]{2,1,0:T(8,128)(2,1)} %bitcast.40, pred[16,72]{1,0:T(8,128)(4,1)S(1)} %broadcast_in_dim.40), kind=kLoop, calls=%fused_computation.6 | loop fusion | flops 2359296 | bytes 9438336 | tf_op jit(solution)/shard_map/jit(_take)/select_n | solution.py:38
  50.4 6.0 %all-to-all-start = ((bf16[16,72,2048]{2,1,0:T(8,128)(2,1)}), bf16[16,72,2048]{2,1,0:T(8,128)(2,1)}, u32[]{:S(2)}, u32[]{:S(2)}) async-start(bf16[16,72,2048]{2,1,0:T(8,128)(2,1)} %broadcast_select_fusion), calls=%async_computation | async-start | bytes 9437184 | tf_op jit(solution)/shard_map/all_to_all | solution.py:46
  56.5 0.7 convert_reduce_fusion
  57.3 102.9 %all-to-all-done = bf16[16,72,2048]{2,1,0:T(8,128)(2,1)} async-done(((bf16[16,72,2048]{2,1,0:T(8,128)(2,1)}), bf16[16,72,2048]{2,1,0:T(8,128)(2,1)}, u32[]{:S(2)}, u32[]{:S(2)}) %all-to-all-start) | async-done | bytes 4718624 | tf_op jit(solution)/shard_map/all_to_all | solution.py:46
  160.2 6.8 %fusion.5 = f32[1152,768]{1,0:T(8,128)S(1)} fusion(bf16[1152,2048]{1,0:T(8,128)(2,1)} %bitcast.2, bf16[1,2048,768]{2,1,0:T(8,128)(2,1)} %param.9), kind=kOutput, calls=%fused_computation.13 | convolution fusion | flops 3623878656 | bytes 11403264 | tf_op jit(solution)/shard_map/dot_general | solution.py:8
  166.9 6.5 %fusion.1 = bf16[1152,768]{1,0:T(8,128)(2,1)S(1)} fusion(bf16[1152,2048]{1,0:T(8,128)(2,1)} %bitcast.2, f32[1152,768]{1,0:T(8,128)S(1)} %fusion.5, bf16[1,2048,768]{2,1,0:T(8,128)(2,1)S(1)} %copy-done.5), kind=kOutput, calls=%fused_computation.8 | convolution fusion | flops 3629187072 | bytes 13172736 | tf_op jit(solution)/shard_map/dot_general | solution.py:9
  173.5 5.6 %fusion = bf16[1152,2048]{1,0:T(8,128)(2,1)} fusion(bf16[1152,768]{1,0:T(8,128)(2,1)S(1)} %fusion.1, f32[1152]{0:T(1024)S(1)} %reshape.130, bf16[1,768,2048]{2,1,0:T(8,128)(2,1)S(1)} %copy-done), kind=kOutput, calls=%fused_computation.5 | convolution fusion | flops 3628597248 | bytes 9638400 | tf_op jit(solution)/shard_map/dot_general | solution.py:11
  179.0 4.9 %all-to-all-start.2 = ((bf16[16,72,2048]{2,1,0:T(8,128)(2,1)}), bf16[16,72,2048]{2,1,0:T(8,128)(2,1)}, u32[]{:S(2)}, u32[]{:S(2)}) async-start(bf16[16,72,2048]{2,1,0:T(8,128)(2,1)} %bitcast.41), calls=%async_computation.2 | async-start | bytes 9437184 | tf_op jit(solution)/shard_map/all_to_all | solution.py:50
  184.2 103.4 %all-to-all-done.2 = bf16[16,72,2048]{2,1,0:T(8,128)(2,1)} async-done(((bf16[16,72,2048]{2,1,0:T(8,128)(2,1)}), bf16[16,72,2048]{2,1,0:T(8,128)(2,1)}, u32[]{:S(2)}, u32[]{:S(2)}) %all-to-all-start.2) | async-done | bytes 4718624 | tf_op jit(solution)/shard_map/all_to_all | solution.py:50
  287.6 10.0 %gather_fusion.2 = bf16[768,2048]{1,0:T(8,128)(2,1)} fusion(bf16[1152,2048]{1,0:T(8,128)(2,1)} %bitcast.7, s32[1024]{0:T(1024)S(1)} %pad_clamp_fusion.2), kind=kCustom, calls=%fused_computation.2 | custom fusion | bytes 6294528 | tf_op jit(solution)/shard_map/jit(_take)/gather | solution.py:52
  297.7 4.3 %fusion.2 = bf16[96,2048]{1,0:T(8,128)(2,1)} fusion(bf16[768,2048]{1,0:T(8,128)(2,1)} %gather_fusion.2, pred[96,8]{1,0:T(8,128)(4,1)S(1)} %copy.23), kind=kLoop, calls=%fused_computation.10 | loop fusion | flops 2949120 | bytes 3539712 | tf_op jit(solution)/shard_map/reduce_sum | solution.py:53
  (24 shorter events, 1.0 us)
Async XLA Ops:
  0.0 173.5 %copy-start = (bf16[1,768,2048]{2,1,0:T(8,128)(2,1)S(1)}, bf16[1,768,2048]{2,1,0:T(8,128)(2,1)}, u32[]{:S(2)}) copy-start(bf16[1,768,2048]{2,1,0:T(8,128)(2,1)} %param.11) | copy-start | bytes 9437188
  0.0 39.5 %copy-start.1 = (bf16[96,2048]{1,0:T(8,128)(2,1)S(1)}, bf16[96,2048]{1,0:T(8,128)(2,1)}, u32[]{:S(2)}) copy-start(bf16[96,2048]{1,0:T(8,128)(2,1)} %param.6) | copy-start | bytes 1179652
  13.0 4.8 %copy-start.3 = (s32[768]{0:T(1024)}, s32[768]{0:T(1024)S(1)}, u32[]{:S(2)}) copy-start(s32[768]{0:T(1024)S(1)} %fusion.15) | copy-start | bytes 9220
  31.6 18.8 %all-to-all-start.1 = ((bf16[16,1,72]{2,1,0:T(2,128)(2,1)}), bf16[16,1,72]{2,1,0:T(2,128)(2,1)}, u32[]{:S(2)}, u32[]{:S(2)}) async-start(bf16[16,1,72]{2,1,0:T(2,128)(2,1)} %select_n.65), calls=%async_computation.1 | async-start | bytes 16384 | tf_op jit(solution)/shard_map/all_to_all | solution.py:47
  50.4 109.7 %all-to-all-start = ((bf16[16,72,2048]{2,1,0:T(8,128)(2,1)}), bf16[16,72,2048]{2,1,0:T(8,128)(2,1)}, u32[]{:S(2)}, u32[]{:S(2)}) async-start(bf16[16,72,2048]{2,1,0:T(8,128)(2,1)} %broadcast_select_fusion), calls=%async_computation | async-start | bytes 9437184 | tf_op jit(solution)/shard_map/all_to_all | solution.py:46
  160.2 6.8 %copy-start.5 = (bf16[1,2048,768]{2,1,0:T(8,128)(2,1)S(1)}, bf16[1,2048,768]{2,1,0:T(8,128)(2,1)}, u32[]{:S(2)}) copy-start(bf16[1,2048,768]{2,1,0:T(8,128)(2,1)} %param.10) | copy-start | bytes 9437188
  179.0 5.1 %copy-start.2 = (s32[96,8]{0,1:T(8,128)S(1)}, s32[96,8]{0,1:T(8,128)}, u32[]{:S(2)}) copy-start(s32[96,8]{0,1:T(8,128)} %param.7) | copy-start | bytes 9220
  179.0 5.2 %copy-start.4 = (s32[768]{0:T(1024)S(1)}, s32[768]{0:T(1024)}, u32[]{:S(2)}) copy-start(s32[768]{0:T(1024)} %copy-done.3) | copy-start | bytes 9220
  179.0 108.6 %all-to-all-start.2 = ((bf16[16,72,2048]{2,1,0:T(8,128)(2,1)}), bf16[16,72,2048]{2,1,0:T(8,128)(2,1)}, u32[]{:S(2)}, u32[]{:S(2)}) async-start(bf16[16,72,2048]{2,1,0:T(8,128)(2,1)} %bitcast.41), calls=%async_computation.2 | async-start | bytes 9437184 | tf_op jit(solution)/shard_map/all_to_all | solution.py:50
where the time goes:
time: 303 us; the launch traced here: 302 us
  waiting for transfers between devices  206 us (68%)
  local copies, waits for them, and re-layouts  41.1 us (14%)
  matrix products  18.8 us (6%)
  other arithmetic  18.1 us (6%)
  starting transfers between devices  17.5 us (6%)
    all_to_all x1, waiting for transfers between devices, local(): back = lax.all_to_all(output, 'ep', split_axis=0, concat_axis=0, tiled=True)  103 us
    all_to_all x1, waiting for transfers between devices, local(): lax.all_to_all(send_rows, 'ep', split_axis=0, concat_axis=0, tiled=True)  103 us
    gather x1, local copies, waits for them, and re-layouts, local(): jnp.take(combine_weights.reshape(-1), owner, mode='fill', fill_value=0)  10.3 us
    gather x1, local copies, waits for them, and re-layouts, local(): per_pair = jnp.take(back_rows, slot_index, axis=0)  10 us
    dot_general x1, matrix products, expert_ffn(): gate = jnp.dot(rows, gate_matrix, preferred_element_type=jnp.float32)  6.76 us
    all_to_all x1, starting transfers between devices, local(): lax.all_to_all(send_weight, 'ep', split_axis=0, concat_axis=0, tiled=True)  6.52 us
    dot_general x1, matrix products, expert_ffn(): upward = jnp.dot(rows, upward_matrix, preferred_element_type=jnp.float32)  6.51 us
  transfers between devices with their start and end apart: 3, of which 2 were waited for; matrix products, arithmetic and copies ran while one was open for 4% of the time, Pallas kernels for 0%

commit v1 on v0

--- a/solution.py
+++ b/solution.py
@@ -1,7 +1,219 @@
+import functools
+
 import jax
 import jax.numpy as jnp
 from jax import lax
+from jax.experimental import pallas as pl
+from jax.experimental.pallas import tpu as pltpu
 from jax.sharding import PartitionSpec as P
+
+MESH = pl.DeviceIdType.MESH
+
+
+def fused_kernel(X, C, x_ref, wg_hbm, wu_hbm, wd_hbm, out_ref,
+                 xall, yall, ysib, acc, arr, wg, wu, wd, hid,
+                 w_sem, own_sem, xs_sem, xr_sem, ps_sem, pr_sem,
+                 ys_sem, yr_sem, as_sem, ar_sem):
+    Z = C // X
+    N = C
+    idx = lax.axis_index("ep")
+    lane = idx % 2
+    chip = idx // 2
+    cx = chip % X
+    cz = chip // X
+    place = cx * Z + cz + (cx % 2) * (Z - 1 - 2 * cz)
+
+    def device_at(r):
+        x = r // Z
+        t = r % Z
+        z = t + (x % 2) * (Z - 1 - 2 * t)
+        return (z * X + x) * 2 + lane
+
+    right = device_at((place + 1) % C)
+    left = device_at((place + C - 1) % C)
+    other = idx + 1 - 2 * lane
+
+    for src, dst, k in ((wg_hbm, wg, 0), (wu_hbm, wu, 1), (wd_hbm, wd, 2)):
+        pltpu.make_async_copy(src.at[0], dst, w_sem.at[k]).start()
+    own = pltpu.make_async_copy(x_ref, xall.at[0, lane], own_sem)
+    own.start()
+
+    barrier = pltpu.get_barrier_semaphore()
+    for peer in (left, right, other):
+        pl.semaphore_signal(barrier, inc=1, device_id={"ep": peer}, device_id_type=MESH)
+    pl.semaphore_wait(barrier, 3)
+
+    ahead = (right, left)
+    behind = (left, right)
+
+    def remote(src, dst, s, r, peer):
+        return pltpu.make_async_remote_copy(
+            src_ref=src, dst_ref=dst, send_sem=s, recv_sem=r,
+            device_id={"ep": peer}, device_id_type=MESH)
+
+    def token_copy(i, d):
+        return remote(x_ref.at[min(i, 2) - 1], xall.at[i, lane, d], xs_sem.at[i, d], xr_sem.at[i, d], ahead[d])
+
+    def pair_copy(i):
+        src = x_ref if i == 0 else xall.at[i, lane]
+        return remote(src, xall.at[i, lane], ps_sem.at[i], pr_sem.at[i], other)
+
+    def partial_copy(i):
+        return remote(yall.at[i, 1 - lane], ysib.at[i], ys_sem.at[i], yr_sem.at[i], other)
+
+    def sum_copy(i, d):
+        return remote(acc.at[i, d], arr.at[i, d], as_sem.at[i, d], ar_sem.at[i, d], behind[d])
+
+    def continues(i, d):
+        if i + 2 < N - 1:
+            return True
+        if i + 2 == N - 1:
+            return d == 0
+        if i + 2 == N:
+            return d == 1
+        return False
+
+    def next_unit(i, d):
+        return i + 2 if i + 2 <= N - 1 else N - 1
+
+    def forward(i, d):
+        k = next_unit(i, d)
+        return remote(xall.at[i, lane, d], xall.at[k, lane, d],
+                      xs_sem.at[k, d], xr_sem.at[k, d], ahead[d])
+
+    width = wg.shape[0]
+    hidden = wg.shape[1]
+    half = x_ref.shape[1]
+    rows = 4 * half
+    ft = 256 if hidden % 256 == 0 else 128
+    nt = 512 if width % 512 == 0 else 128
+
+    def ffn(i):
+        xw = xall[i, :, :, :, width:].reshape(rows, xall.shape[-1] - width).astype(jnp.float32)
+        pick = lax.broadcasted_iota(jnp.int32, xw.shape, 1) == idx
+        scale = jnp.sum(jnp.where(pick, xw, 0.0), axis=1, keepdims=True)
+
+        @pl.loop(0, hidden // ft)
+        def _(f):
+            cols = pl.ds(pl.multiple_of(f * ft, ft), ft)
+            xv = xall[i, :, :, :, :width].reshape(rows, width)
+            g = jnp.dot(xv, wg[:, cols], preferred_element_type=jnp.float32)
+            u = jnp.dot(xv, wu[:, cols], preferred_element_type=jnp.float32)
+            hid[:, cols] = (g / (1.0 + jnp.exp(-g)) * u).astype(jnp.bfloat16)
+
+        @pl.loop(0, width // nt)
+        def _(n):
+            cols = pl.ds(pl.multiple_of(n * nt, nt), nt)
+            y = jnp.dot(hid[...], wd[:, cols], preferred_element_type=jnp.float32) * scale
+            yall[i, :, :, :, cols] = y.astype(jnp.bfloat16).reshape(2, 2, half, nt)
+
+    def reduce_send(i, d):
+        total = yall[i, lane, d].astype(jnp.float32) + ysib[i, d].astype(jnp.float32)
+        if continues(i, d):
+            k = next_unit(i, d)
+            sum_copy(k, d).wait_recv()
+            total = total + arr[k, d].astype(jnp.float32)
+        acc[i, d] = total.astype(jnp.bfloat16)
+        sum_copy(i, d).start()
+
+    for i in (1, 2):
+        for d in (0, 1):
+            token_copy(i, d).start()
+    pair_copy(0).start()
+
+    for i in range(N):
+        if i > 0:
+            for d in (0, 1):
+                token_copy(i, d).wait_recv()
+                if continues(i, d):
+                    forward(i, d).start()
+            pair_copy(i).start()
+        else:
+            own.wait()
+            for src, dst, k in ((wg_hbm, wg, 0), (wu_hbm, wu, 1), (wd_hbm, wd, 2)):
+                pltpu.make_async_copy(src.at[0], dst, w_sem.at[k]).wait()
+        remote(xall.at[i, lane], xall.at[i, 1 - lane], ps_sem.at[i], pr_sem.at[i], other).wait_recv()
+        if i == N - 1:
+            partial_copy(N - 2).wait_recv()
+            reduce_send(N - 2, 0)
+        ffn(i)
+        partial_copy(i).start()
+        if i == N - 2:
+            partial_copy(N - 3).wait_recv()
+            reduce_send(N - 3, 1)
+
+    for i in range(N - 3):
+        partial_copy(i).wait_recv()
+    partial_copy(N - 1).wait_recv()
+    reduce_send(N - 1, 0)
+    reduce_send(N - 1, 1)
+    order = ([], [])
+    for d in (0, 1):
+        a, b = (N - 4, N - 3) if d == 0 else (N - 5, N - 2)
+        while a >= 1 or b >= 1:
+            if a >= 1:
+                order[d].append(a)
+            if b >= 1:
+                order[d].append(b)
+            a, b = a - 2, b - 2
+    for s in range(max(len(order[0]), len(order[1]))):
+        for d in (0, 1):
+            if s < len(order[d]):
+                reduce_send(order[d][s], d)
+
+    for h in (0, 1):
+        total = yall[0, lane, h].astype(jnp.float32) + ysib[0, h].astype(jnp.float32)
+        for d in (0, 1):
+            sum_copy(h + 1, d).wait_recv()
+            total = total + arr[h + 1, d].astype(jnp.float32)
+        out_ref[h] = total.astype(out_ref.dtype)
+
+    for i in range(N):
+        pair_copy(i).wait_send()
+        partial_copy(i).wait_send()
+        if i > 0:
+            for d in (0, 1):
+                token_copy(i, d).wait_send()
+                sum_copy(i, d).wait_send()
+
+
+def fused_local(X, tokens, routes, combine_weights, w_gate, w_up, w_down):
+    peers = lax.axis_size("ep")
+    local_tokens, width = tokens.shape
+    hidden = w_gate.shape[2]
+    C = peers // 2
+    half = local_tokens // 2
+    pad = -(-peers // 128) * 128
+    names = jnp.arange(pad, dtype=jnp.int32)
+    dense = jnp.sum(
+        jnp.where(routes[:, :, None] == names[None, None, :],
+                  combine_weights[:, :, None].astype(jnp.float32), 0.0), axis=1)
+    x = jnp.concatenate([tokens, dense.astype(jnp.bfloat16)], axis=1)
+    x = x.reshape(2, half, width + pad)
+    bf = jnp.bfloat16
+    dma = pltpu.SemaphoreType.DMA
+    out = pl.pallas_call(
+        functools.partial(fused_kernel, X, C),
+        out_shape=jax.ShapeDtypeStruct((2, half, width), bf),
+        in_specs=[pl.BlockSpec(memory_space=pltpu.VMEM)] + [pl.BlockSpec(memory_space=pl.ANY)] * 3,
+        out_specs=pl.BlockSpec(memory_space=pltpu.VMEM),
+        scratch_shapes=[
+            pltpu.VMEM((C, 2, 2, half, width + pad), bf),
+            pltpu.VMEM((C, 2, 2, half, width), bf),
+            pltpu.VMEM((C, 2, half, width), bf),
+            pltpu.VMEM((C, 2, half, width), bf),
+            pltpu.VMEM((C, 2, half, width), bf),
+            pltpu.VMEM((width, hidden), bf),
+            pltpu.VMEM((width, hidden), bf),
+            pltpu.VMEM((hidden, width), bf),
+            pltpu.VMEM((4 * half, hidden), bf),
+            dma((3,)), dma,
+            dma((C, 2)), dma((C, 2)), dma((C,)), dma((C,)),
+            dma((C,)), dma((C,)), dma((C, 2)), dma((C, 2)),
+        ],
+        compiler_params=pltpu.CompilerParams(collective_id=0, has_side_effects=True),
+    )(x, w_gate, w_up, w_down)
+    return out.reshape(local_tokens, width)
 
 
 def expert_ffn(rows, row_weight, gate_matrix, upward_matrix, down_matrix):
@@ -64,4 +276,12 @@
         P("ep", None, None),
     )
     out_specs = P(("dp", "ep"), None)
-    return jax.shard_map(local, mesh=mesh, in_specs=in_specs, out_specs=out_specs, check_vma=False)
+    peers, X = mesh.shape["ep"], mesh.shape["dp"]
+
+    def layer(tokens, routes, *rest):
+        count = tokens.shape[0]
+        dense = peers <= 2 * routes.shape[1] and peers % (4 * X) == 0 and count % 32 == 0
+        body = functools.partial(fused_local, X) if dense and peers >= 8 else local
+        return body(tokens, routes, *rest)
+
+    return jax.shard_map(layer, mesh=mesh, in_specs=in_specs, out_specs=out_specs, check_vma=False)

time: 303 us -> 87 us (0.29)
  the two profiles are of different devices: /device:TPU:15 before, /device:TPU:0 now
where the time goes in v1:
time: 87 us; the launch traced here: 86.7 us
  Pallas kernels  81.3 us (93%)
  local copies, waits for them, and re-layouts  3.32 us (4%)
  other arithmetic  2.06 us (2%)
    pallas_call x1, Pallas kernels, fused_local(): pl.pallas_call(functools.partial(fused_kernel, X, C), out_shape=jax.Shape...  81.3 us
    unnamed x2, local copies, waits for them, and re-layouts  2.55 us
    concatenate x1, other arithmetic, fused_local(): x = jnp.concatenate([tokens, dense.astype(jnp.bfloat16)], axis=1)  1.77 us

profile of v1, /device:TPU:0, one launch (start us, length us, event | category | flops | bytes accessed | tf_op | source)
XLA Modules:
  0.0 86.7 jit_solution(1926945533996880747)
XLA Ops:
  0.0 0.8 copy.9
  0.8 0.8 copy.10
  1.6 0.3 select_reduce_fusion
  1.8 1.8 %pad_maximum_fusion = bf16[96,2176]{1,0:T(8,128)(2,1)} fusion(bf16[96,128]{1,0:T(8,128)(2,1)S(1)} %select_reduce_fusion, bf16[96,2048]{1,0:T(8,128)(2,1)} %param.6), kind=kLoop, calls=%fused_computation | loop fusion | flops 835584 | bytes 835584 | tf_op jit(solution)/shard_map/concatenate | solution.py:191
  3.6 81.3 %shard_map.64 = bf16[2,48,2048]{2,1,0:T(8,128)(2,1)} custom-call(bf16[2,48,2176]{2,1,0:T(8,128)(2,1)} %bitcast.2, bf16[1,2048,768]{2,1,0:T(8,128)(2,1)} %wg_hbm.1, bf16[1,2048,768]{2,1,0:T(8,128)(2,1)} %wu_hbm.1, bf16[1,768,2048]{2,1,0:T(8,128)(2,1)} %wd_hbm.1), custom_call_target="tpu_custom_call" | custom-call | tf_op jit(solution)/shard_map/pallas_call | solution.py:195
  84.9 1.8 %copy.12 = bf16[96,2048]{1,0:T(8,128)(2,1)} copy(bf16[96,2048]{1,0:T(8,128)(2,1)} %bitcast.3) | data formatting | bytes 786432

commit v2 on v1

--- a/solution.py
+++ b/solution.py
@@ -10,7 +10,7 @@
 MESH = pl.DeviceIdType.MESH
 
 
-def fused_kernel(X, C, x_ref, wg_hbm, wu_hbm, wd_hbm, out_ref,
+def fused_kernel(X, C, x_hbm, c_hbm, wg_hbm, wu_hbm, wd_hbm, out_ref,
                  xall, yall, ysib, acc, arr, wg, wu, wd, hid,
                  w_sem, own_sem, xs_sem, xr_sem, ps_sem, pr_sem,
                  ys_sem, yr_sem, as_sem, ar_sem):
@@ -33,10 +33,19 @@
     left = device_at((place + C - 1) % C)
     other = idx + 1 - 2 * lane
 
-    for src, dst, k in ((wg_hbm, wg, 0), (wu_hbm, wu, 1), (wd_hbm, wd, 2)):
-        pltpu.make_async_copy(src.at[0], dst, w_sem.at[k]).start()
-    own = pltpu.make_async_copy(x_ref, xall.at[0, lane], own_sem)
-    own.start()
+    width = wg.shape[0]
+    half = xall.shape[3]
+    pad = xall.shape[4] - width
+    own = (
+        pltpu.make_async_copy(x_hbm, xall.at[0, lane, :, :, pl.ds(0, width)], own_sem.at[0]),
+        pltpu.make_async_copy(c_hbm, xall.at[0, lane, :, :, pl.ds(width, pad)], own_sem.at[1]),
+    )
+    weights = [pltpu.make_async_copy(src.at[0], dst, w_sem.at[k])
+               for src, dst, k in ((wg_hbm, wg, 0), (wu_hbm, wu, 1), (wd_hbm, wd, 2))]
+    for copy in own:
+        copy.start()
+    for copy in weights:
+        copy.start()
 
     barrier = pltpu.get_barrier_semaphore()
     for peer in (left, right, other):
@@ -52,11 +61,10 @@
             device_id={"ep": peer}, device_id_type=MESH)
 
     def token_copy(i, d):
-        return remote(x_ref.at[min(i, 2) - 1], xall.at[i, lane, d], xs_sem.at[i, d], xr_sem.at[i, d], ahead[d])
+        return remote(xall.at[0, lane, min(i, 2) - 1], xall.at[i, lane, d], xs_sem.at[i, d], xr_sem.at[i, d], ahead[d])
 
     def pair_copy(i):
-        src = x_ref if i == 0 else xall.at[i, lane]
-        return remote(src, xall.at[i, lane], ps_sem.at[i], pr_sem.at[i], other)
+        return remote(xall.at[i, lane], xall.at[i, lane], ps_sem.at[i], pr_sem.at[i], other)
 
     def partial_copy(i):
         return remote(yall.at[i, 1 - lane], ysib.at[i], ys_sem.at[i], yr_sem.at[i], other)
@@ -81,31 +89,19 @@
         return remote(xall.at[i, lane, d], xall.at[k, lane, d],
                       xs_sem.at[k, d], xr_sem.at[k, d], ahead[d])
 
-    width = wg.shape[0]
-    hidden = wg.shape[1]
-    half = x_ref.shape[1]
     rows = 4 * half
-    ft = 256 if hidden % 256 == 0 else 128
-    nt = 512 if width % 512 == 0 else 128
 
     def ffn(i):
-        xw = xall[i, :, :, :, width:].reshape(rows, xall.shape[-1] - width).astype(jnp.float32)
+        xw = xall[i, :, :, :, width:].reshape(rows, pad).astype(jnp.float32)
         pick = lax.broadcasted_iota(jnp.int32, xw.shape, 1) == idx
         scale = jnp.sum(jnp.where(pick, xw, 0.0), axis=1, keepdims=True)
 
-        @pl.loop(0, hidden // ft)
-        def _(f):
-            cols = pl.ds(pl.multiple_of(f * ft, ft), ft)
-            xv = xall[i, :, :, :, :width].reshape(rows, width)
-            g = jnp.dot(xv, wg[:, cols], preferred_element_type=jnp.float32)
-            u = jnp.dot(xv, wu[:, cols], preferred_element_type=jnp.float32)
-            hid[:, cols] = (g / (1.0 + jnp.exp(-g)) * u).astype(jnp.bfloat16)
-
-        @pl.loop(0, width // nt)
-        def _(n):
-            cols = pl.ds(pl.multiple_of(n * nt, nt), nt)
-            y = jnp.dot(hid[...], wd[:, cols], preferred_element_type=jnp.float32) * scale
-            yall[i, :, :, :, cols] = y.astype(jnp.bfloat16).reshape(2, 2, half, nt)
+        xv = xall[i, :, :, :, :width].reshape(rows, width)
+        g = jnp.dot(xv, wg[...], preferred_element_type=jnp.float32)
+        u = jnp.dot(xv, wu[...], preferred_element_type=jnp.float32)
+        hid[...] = (g / (1.0 + jnp.exp(-g)) * u).astype(jnp.bfloat16)
+        y = jnp.dot(hid[...], wd[...], preferred_element_type=jnp.float32) * scale
+        yall[i] = y.astype(jnp.bfloat16).reshape(2, 2, half, width)
 
     def reduce_send(i, d):
         total = yall[i, lane, d].astype(jnp.float32) + ysib[i, d].astype(jnp.float32)
@@ -116,6 +112,8 @@
         acc[i, d] = total.astype(jnp.bfloat16)
         sum_copy(i, d).start()
 
+    for copy in own:
+        copy.wait()
     for i in (1, 2):
         for d in (0, 1):
             token_copy(i, d).start()
@@ -129,9 +127,8 @@
                     forward(i, d).start()
             pair_copy(i).start()
         else:
-            own.wait()
-            for src, dst, k in ((wg_hbm, wg, 0), (wu_hbm, wu, 1), (wd_hbm, wd, 2)):
-                pltpu.make_async_copy(src.at[0], dst, w_sem.at[k]).wait()
+            for copy in weights:
+                copy.wait()
         remote(xall.at[i, lane], xall.at[i, 1 - lane], ps_sem.at[i], pr_sem.at[i], other).wait_recv()
         if i == N - 1:
             partial_copy(N - 2).wait_recv()
@@ -188,14 +185,14 @@
     dense = jnp.sum(
         jnp.where(routes[:, :, None] == names[None, None, :],
                   combine_weights[:, :, None].astype(jnp.float32), 0.0), axis=1)
-    x = jnp.concatenate([tokens, dense.astype(jnp.bfloat16)], axis=1)
-    x = x.reshape(2, half, width + pad)
+    dense = dense.astype(jnp.bfloat16).reshape(2, half, pad)
+    x = tokens.reshape(2, half, width)
     bf = jnp.bfloat16
     dma = pltpu.SemaphoreType.DMA
     out = pl.pallas_call(
         functools.partial(fused_kernel, X, C),
         out_shape=jax.ShapeDtypeStruct((2, half, width), bf),
-        in_specs=[pl.BlockSpec(memory_space=pltpu.VMEM)] + [pl.BlockSpec(memory_space=pl.ANY)] * 3,
+        in_specs=[pl.BlockSpec(memory_space=pl.ANY)] * 5,
         out_specs=pl.BlockSpec(memory_space=pltpu.VMEM),
         scratch_shapes=[
             pltpu.VMEM((C, 2, 2, half, width + pad), bf),
@@ -207,12 +204,12 @@
             pltpu.VMEM((width, hidden), bf),
             pltpu.VMEM((hidden, width), bf),
             pltpu.VMEM((4 * half, hidden), bf),
-            dma((3,)), dma,
+            dma((3,)), dma((2,)),
             dma((C, 2)), dma((C, 2)), dma((C,)), dma((C,)),
             dma((C,)), dma((C,)), dma((C, 2)), dma((C, 2)),
         ],
         compiler_params=pltpu.CompilerParams(collective_id=0, has_side_effects=True),
-    )(x, w_gate, w_up, w_down)
+    )(x, dense, w_gate, w_up, w_down)
     return out.reshape(local_tokens, width)
 
 

time: 87 us -> 82.7 us (0.951)
  Pallas kernels: 81.3 us -> 78.3 us
  other arithmetic: 2.06 us -> 0.9 us
    pallas_call x1, Pallas kernels: 81.3 us -> 78.3 us  [fused_local(): pl.pallas_call(functools.partial(fused_kernel, X, C), out_shape=jax.Shape...]
    concatenate x1 -> x0, other arithmetic: 1.77 us -> none  [fused_local(): x = jnp.concatenate([tokens, dense.astype(jnp.bfloat16)], axis=1)]
where the time goes in v2:
time: 82.7 us; the launch traced here: 82.5 us
  Pallas kernels  78.3 us (95%)
  local copies, waits for them, and re-layouts  3.32 us (4%)
  other arithmetic  0.9 us (1%)
    pallas_call x1, Pallas kernels, fused_local(): pl.pallas_call(functools.partial(fused_kernel, X, C), out_shape=jax.Shape...  78.3 us
    unnamed x2, local copies, waits for them, and re-layouts  2.55 us

profile of v2, /device:TPU:0, one launch (start us, length us, event | category | flops | bytes accessed | tf_op | source)
XLA Modules:
  0.0 82.5 jit_solution(5985394729884192526)
XLA Ops:
  0.0 0.8 copy.9
  0.8 0.8 copy.10
  1.6 0.9 %select_reduce_fusion = bf16[96,128]{1,0:T(8,128)(2,1)} fusion(f32[96,8]{1,0:T(8,128)S(1)} %copy.10, s32[96,8]{1,0:T(8,128)S(1)} %copy.9), kind=kLoop, calls=%fused_computation | loop fusion | flops 282624 | bytes 30720 | tf_op jit(solution)/shard_map/reduce_sum | solution.py:185
  2.5 78.3 %shard_map.64 = bf16[2,48,2048]{2,1,0:T(8,128)(2,1)} custom-call(bf16[2,48,2048]{2,1,0:T(8,128)(2,1)} %bitcast.4, bf16[2,48,128]{2,1,0:T(8,128)(2,1)} %bitcast.5, bf16[1,2048,768]{2,1,0:T(8,128)(2,1)} %wg_hbm.1, bf16[1,2048,768]{2,1,0:T(8,128)(2,1)} %wu_hbm.1, bf16[1,768,2048]{2,1,0:T(8,128)(2,1)} %wd_hbm.1), custom_call_target="tpu_custom_call" | custom-call | tf_op jit(solution)/shard_map/pallas_call | solution.py:192
  80.7 1.8 %copy.12 = bf16[96,2048]{1,0:T(8,128)(2,1)} copy(bf16[96,2048]{1,0:T(8,128)(2,1)} %bitcast.3) | data formatting | bytes 786432
